TPU v7x, 256 devices: a whole 4x4x8 slice. The times are simulated.
256 devices in a mesh: mp: 64 (over z, x, core), head: 4 (over y).
Axes of the slice: x: 4, y: 4, z: 8, core: 2. Of those that a mesh axis runs over, the one named last changes fastest.
Arguments:
- hidden: bfloat16 [8, 4096], replicated, may hold values from -6 to 6
- norm_gain: float32 [4096], replicated, may hold values from 0.25 to 1.75
- w_query: bfloat16 [4096, 4096], P('mp', 'head'), may hold values from -0.09375 to 0.09375
- enc_states: bfloat16 [8, 4096, 4096], P(None, 'mp'), may hold values from -6 to 6
- w_key: bfloat16 [4096, 4096], P('mp', 'head'), may hold values from -0.09375 to 0.09375
- w_value: bfloat16 [4096, 4096], P('mp', 'head'), may hold values from -0.09375 to 0.09375
- w_out: bfloat16 [4096, 4096], P('head', 'mp'), may hold values from -0.09375 to 0.09375
- bias_table: float32 [32, 64], P(None, 'head'), may hold values from -5 to 300
- buckets: int32 [8, 4096], P(None, 'mp'), may hold values from 0 to 31
- src_len: int32 [8], replicated, may hold values from 512 to 4096
Outputs:
- updated: bfloat16 [8, 4096], P(None, 'mp')
All inputs are finite; a program needn't handle non-finite values.
Results may differ from a plain program's by a relative error of at most 0.0049.
Values may be sent and summed in bfloat16 or wider, within the bound.
A program may use at most 128 MiB of HBM per device.

v0:
```python
import jax
import jax.numpy as jnp
from jax import lax
from jax.sharding import PartitionSpec as P

EPSILON = 1e-06
NEGATIVE = -1e30


def shards(
    hidden, norm_gain, w_query, enc_states, w_key, w_value, w_out, bias_table, buckets, src_len
):
    batch, src_local, _ = enc_states.shape
    rows, inner = w_key.shape
    heads = bias_table.shape[1]
    head_size = inner // heads
    me = lax.axis_index("mp")
    widened = hidden.astype(jnp.float32)
    mean_square = jnp.mean(widened * widened, axis=-1, keepdims=True)
    normed = (widened * lax.rsqrt(mean_square + EPSILON) * norm_gain).astype(jnp.bfloat16)
    mine = lax.dynamic_slice_in_dim(normed, me * rows, rows, 1)
    query = jnp.dot(mine, w_query, preferred_element_type=jnp.float32)
    query = lax.psum(query, "mp").astype(jnp.bfloat16).reshape(batch, heads, head_size)
    probe = jnp.einsum(
        "bhe,dhe->bhd",
        query,
        w_key.reshape(rows, heads, head_size),
        preferred_element_type=jnp.float32,
    )
    probe = (probe * float(head_size) ** (-0.5)).astype(jnp.bfloat16)
    probe = lax.all_gather(probe, "mp", axis=2, tiled=True)
    scores = jnp.einsum("bhd,bsd->bhs", probe, enc_states, preferred_element_type=jnp.float32)
    ids = jnp.arange(bias_table.shape[0], dtype=jnp.int32)
    one_hot = (buckets[:, :, None] == ids[None, None, :]).astype(jnp.float32)
    scores = scores + jnp.einsum(
        "bsk,kh->bhs", one_hot, bias_table, precision=lax.Precision.HIGHEST
    )
    positions = me * src_local + jnp.arange(src_local, dtype=jnp.int32)
    live = (positions[None, :] < src_len[:, None])[:, None, :]
    scores = jnp.where(live, scores, NEGATIVE)
    top = lax.pmax(jnp.max(scores, axis=-1), "mp")
    weights = jnp.where(live, jnp.exp(scores - top[:, :, None]), 0.0)
    total = lax.psum(jnp.sum(weights, axis=-1), "mp")
    mixed = jnp.einsum(
        "bhs,bsd->bhd", weights.astype(jnp.bfloat16), enc_states, preferred_element_type=jnp.float32
    )
    mixed = lax.psum_scatter(mixed, "mp", scatter_dimension=2, tiled=True)
    mixed = (mixed / total[:, :, None]).astype(jnp.bfloat16)
    context = jnp.einsum(
        "bhd,dhe->bhe",
        mixed,
        w_value.reshape(rows, heads, head_size),
        preferred_element_type=jnp.float32,
    )
    context = lax.psum(context, "mp").astype(jnp.bfloat16).reshape(batch, inner)
    out = lax.psum(jnp.dot(context, w_out, preferred_element_type=jnp.float32), "head")
    cols = w_out.shape[1]
    residual = lax.dynamic_slice_in_dim(widened, me * cols, cols, 1)
    return (out + residual).astype(jnp.bfloat16)


def solution(mesh):
    in_specs = (
        P(),
        P(),
        P("mp", "head"),
        P(None, "mp", None),
        P("mp", "head"),
        P("mp", "head"),
        P("head", "mp"),
        P(None, "head"),
        P(None, "mp"),
        P(),
    )
    return jax.shard_map(
        shards, mesh=mesh, in_specs=in_specs, out_specs=P(None, "mp"), check_vma=False
    )
```

profile of v0, /device:TPU:0, one launch (start us, length us, event | category | flops | bytes accessed | tf_op | source)
XLA Modules:
  0.0 922.8 jit_solution(14839864621208806205)
XLA Ops:
  6.5 0.9 convert_element_type.28
  7.4 1.0 multiply_reduce_fusion
  8.4 0.8 dynamic-slice
  9.2 0.2 fusion.19
  9.4 251.9 %psum.28 = bf16[8,1024]{1,0:T(8,128)(2,1)S(1)} all-reduce(f32[8,1024]{1,0:T(8,128)S(1)} %fusion.19), channel_id=1, replica_groups=mesh['mp'=64,'head'=4] {'mp'}, use_global_device_ids=true, to_apply=%region_1.0 | all-reduce | flops 8192 | bytes 49152 | tf_op jit(solution)/shard_map/psum | solution.py:23
  261.4 1.1 reshape.52
  262.5 0.3 fusion.5
  262.7 0.8 copy.16
  263.6 0.7 broadcast_compare_fusion
  264.4 77.1 %all-gather.2.cloned.1.call-done = bf16[8,16,4096]{1,0,2:T(8,128)(2,1)} async-done(((bf16[8,16,64]{1,0,2:T(8,128)(2,1)}), bf16[8,16,4096]{1,0,2:T(8,128)(2,1)}) %all-gather.2.cloned.1.call-update) | async-done | bytes 1048592 | tf_op jit(solution)/shard_map/all_gather | solution.py:31
  341.5 7.3 fusion
  348.8 0.3 fusion.24
  349.1 126.0 %pmax.7 = f32[8,16]{1,0:T(8,128)S(1)} all-reduce(f32[8,16]{1,0:T(8,128)S(1)} %get-tuple-element.5), channel_id=1, replica_groups=mesh['mp'=64,'head'=4] {'mp'}, use_global_device_ids=true, to_apply=%region_3.4 | all-reduce | flops 128 | bytes 1024 | tf_op jit(solution)/shard_map/pmax | solution.py:41
  475.1 2.9 fusion.11
  478.0 16.8 %copy.22 = f32[8,16,4096]{0,1,2:T(8,128)} copy(f32[8,16,4096]{2,1,0:T(8,128)S(1)} %fusion.11) | data formatting | bytes 4194304
  494.8 23.7 %reshape.56 = f32[4096,128]{1,0:T(8,128)} reshape(f32[4096,16,8]{2,1,0:T(8,128)} %bitcast.23) | data formatting | bytes 4194304
  518.9 124.3 %psum.29 = f32[8,16]{1,0:T(8,128)S(1)} all-reduce(f32[8,16]{1,0:T(8,128)S(1)} %fusion.9), channel_id=1, replica_groups=mesh['mp'=64,'head'=4] {'mp'}, use_global_device_ids=true, to_apply=%region_6.7 | all-reduce | flops 128 | bytes 1024 | tf_op jit(solution)/shard_map/psum | solution.py:43
  643.3 13.6 %reduce-scatter.4.cloned.1.call-done = f32[64,128]{1,0:T(8,128)} async-done(((f32[4096,128]{1,0:T(8,128)}), f32[64,128]{1,0:T(8,128)}) %reduce-scatter.4.cloned.1.call-update) | async-done | bytes 32784
  656.9 1.0 reshape.57
  658.0 0.2 copy.23
  658.2 0.2 convolution_bitcast_fusion
  658.5 246.1 %psum.30 = bf16[8,16,64]{2,0,1:T(8,128)(2,1)S(1)} all-reduce(f32[8,16,64]{2,0,1:T(8,128)S(1)} %convolution_bitcast_fusion), channel_id=1, replica_groups=mesh['mp'=64,'head'=4] {'mp'}, use_global_device_ids=true, to_apply=%region_7.8 | all-reduce | flops 8192 | bytes 49152 | tf_op jit(solution)/shard_map/psum | solution.py:55
  904.9 10.5 %psum.31 = f32[8,64]{1,0:T(8,128)S(1)} all-reduce(f32[8,64]{1,0:T(8,128)S(1)} %fusion.25), channel_id=1, replica_groups=mesh['mp'=64,'head'=4] {'head'}, use_global_device_ids=true, to_apply=%region_8.9 | all-reduce | flops 512 | bytes 4096 | tf_op jit(solution)/shard_map/psum | solution.py:56
  915.3 0.7 add_convert_fusion
  (23 shorter events, 0.9 us)
Async XLA Ops:
  6.5 2.7 copy-start
  6.5 334.9 %all-gather.2.cloned.1.call-start = ((), (), s32[]{:S(2)}) async-start(), calls=%async_computation.1 | async-start | bytes 8519680 | tf_op jit(solution)/shard_map/all_gather | solution.py:31
  263.6 393.4 %reduce-scatter.4.cloned.1.call-start = ((), (), s32[]{:S(2)}) async-start(), calls=%async_computation.2 | async-start | bytes 2129920
  264.4 84.4 %copy-start.3 = (f32[32,16]{0,1:T(8,128)S(1)}, f32[32,16]{0,1:T(8,128)}, u32[]{:S(2)}) copy-start(f32[32,16]{0,1:T(8,128)} %param.17) | copy-start | bytes 6148
  264.4 84.4 %copy-start.4 = (s32[8,64]{1,0:T(8,128)S(1)}, s32[8,64]{1,0:T(8,128)}, u32[]{:S(2)}) copy-start(s32[8,64]{1,0:T(8,128)} %param.18) | copy-start | bytes 6148
  494.8 23.7 %copy-start.1 = (bf16[64,1024]{1,0:T(8,128)(2,1)S(1)}, bf16[64,1024]{1,0:T(8,128)(2,1)}, u32[]{:S(2)}) copy-start(bf16[64,1024]{1,0:T(8,128)(2,1)} %param.15) | copy-start | bytes 393220
  518.5 386.2 %copy-start.2 = (bf16[1024,64]{0,1:T(8,128)(2,1)S(1)}, bf16[1024,64]{0,1:T(8,128)(2,1)}, u32[]{:S(2)}) copy-start(bf16[1024,64]{0,1:T(8,128)(2,1)} %param.16) | copy-start | bytes 393220
Sparse Core Ops, SparseCore 0:
  263.7 77.7 all-gather.1
  518.7 138.2 reduce-scatter.3
where the time goes:
time: 924 us; the launch traced here: 923 us
  blocking collectives  759 us (82%)
  waiting for transfers between devices  90.8 us (10%)
  local copies, waits for them, and re-layouts  45 us (5%)
  between operations  13.5 us (1%)
  matrix products  11.3 us (1%)
    psum x1, blocking collectives, shards(): lax.psum(query, 'mp').astype(jnp.bfloat16).reshape(batch, heads, head_size)  252 us
    psum x1, blocking collectives, shards(): context = lax.psum(context, 'mp').astype(jnp.bfloat16).reshape(batch, inner)  246 us
    pmax x1, blocking collectives, shards(): top = lax.pmax(jnp.max(scores, axis=-1), 'mp')  126 us
    psum x1, blocking collectives, shards(): total = lax.psum(jnp.sum(weights, axis=-1), 'mp')  124 us
    all_gather x1, waiting for transfers between devices, shards(): probe = lax.all_gather(probe, 'mp', axis=2, tiled=True)  77.1 us
    unnamed x14, local copies, waits for them, and re-layouts  41.8 us
  transfers between devices with their start and end apart: 2, of which 2 were waited for; matrix products, arithmetic and copies ran while one was open for 0% of the time, Pallas kernels for 0%

commit v1 on v0

--- a/solution.py
+++ b/solution.py
@@ -28,7 +28,8 @@
         preferred_element_type=jnp.float32,
     )
     probe = (probe * float(head_size) ** (-0.5)).astype(jnp.bfloat16)
-    probe = lax.all_gather(probe, "mp", axis=2, tiled=True)
+    before = jnp.concatenate([probe] * lax.psum(1, "mp"), 2)
+    probe = lax.all_to_all(before, axis_name="mp", split_axis=2, concat_axis=2, tiled=True)
     scores = jnp.einsum("bhd,bsd->bhs", probe, enc_states, preferred_element_type=jnp.float32)
     ids = jnp.arange(bias_table.shape[0], dtype=jnp.int32)
     one_hot = (buckets[:, :, None] == ids[None, None, :]).astype(jnp.float32)

time: 924 us -> 907 us (0.982)
  waiting for transfers between devices: 90.8 us -> 42.9 us
  local copies, waits for them, and re-layouts: 45 us -> 73 us
    all_gather x1 -> x0, waiting for transfers between devices: 77.1 us -> none  [shards(): probe = lax.all_gather(probe, 'mp', axis=2, tiled=True)]
    all_to_all x0 -> x1, waiting for transfers between devices: none -> 28.7 us  [shards(): lax.all_to_all(before, axis_name='mp', split_axis=2, concat_axis=2, tiled...]
    unnamed x14 -> x18, local copies, waits for them, and re-layouts: 41.8 us -> 61.8 us
where the time goes in v1:
time: 907 us; the launch traced here: 906 us
  blocking collectives  758 us (84%)
  local copies, waits for them, and re-layouts  73 us (8%)
  waiting for transfers between devices  42.9 us (5%)
  between operations  13.5 us (1%)
  matrix products  11.3 us (1%)
    psum x1, blocking collectives, shards(): lax.psum(query, 'mp').astype(jnp.bfloat16).reshape(batch, heads, head_size)  252 us
    psum x1, blocking collectives, shards(): context = lax.psum(context, 'mp').astype(jnp.bfloat16).reshape(batch, inner)  246 us
    pmax x1, blocking collectives, shards(): top = lax.pmax(jnp.max(scores, axis=-1), 'mp')  125 us
    psum x1, blocking collectives, shards(): total = lax.psum(jnp.sum(weights, axis=-1), 'mp')  124 us
    unnamed x18, local copies, waits for them, and re-layouts  61.8 us
    all_to_all x1, waiting for transfers between devices, shards(): lax.all_to_all(before, axis_name='mp', split_axis=2, concat_axis=2, tiled...  28.7 us
  transfers between devices with their start and end apart: 2, of which 2 were waited for; matrix products, arithmetic and copies ran while one was open for 0% of the time, Pallas kernels for 0%

profile of v1, /device:TPU:0, one launch (start us, length us, event | category | flops | bytes accessed | tf_op | source)
XLA Modules:
  0.0 906.0 jit_solution(3862142294866757458)
XLA Ops:
  6.5 0.9 convert_element_type.28
  7.4 1.0 multiply_reduce_fusion
  8.4 0.8 dynamic-slice
  9.4 251.9 %psum.28 = bf16[8,1024]{1,0:T(8,128)(2,1)S(1)} all-reduce(f32[8,1024]{1,0:T(8,128)S(1)} %fusion.19), channel_id=1, replica_groups=mesh['mp'=64,'head'=4] {'mp'}, use_global_device_ids=true, to_apply=%region_1.0 | all-reduce | flops 8192 | bytes 49152 | tf_op jit(solution)/shard_map/psum | solution.py:23
  261.4 1.1 reshape.52
  262.5 0.2 fusion.5
  262.7 1.4 concatenate.3
  264.2 7.4 copy.16
  271.6 12.5 %reshape.58 = bf16[64,2,4096]{2,1,0:T(2,128)(2,1)} reshape(bf16[4096,8,16]{2,1,0:T(8,128)(2,1)} %bitcast.26) | data formatting | bytes 2097152
  284.0 4.7 all-to-all-start
  288.8 28.7 %all-to-all-done = bf16[64,2,4096]{2,1,0:T(2,128)(2,1)S(1)} async-done(((bf16[64,2,4096]{2,1,0:T(2,128)(2,1)}), bf16[64,2,4096]{2,1,0:T(2,128)(2,1)S(1)}, u32[]{:S(2)}, u32[]{:S(2)}) %all-to-all-start) | async-done | bytes 1048608 | tf_op jit(solution)/shard_map/all_to_all | solution.py:32
  317.6 7.5 reshape.59
  325.1 7.3 fusion
  332.4 0.3 fusion.24
  332.7 125.2 %pmax.7 = f32[8,16]{1,0:T(8,128)S(1)} all-reduce(f32[8,16]{1,0:T(8,128)S(1)} %get-tuple-element.5), channel_id=1, replica_groups=mesh['mp'=64,'head'=4] {'mp'}, use_global_device_ids=true, to_apply=%region_3.4 | all-reduce | flops 128 | bytes 1024 | tf_op jit(solution)/shard_map/pmax | solution.py:42
  457.9 2.9 fusion.11
  460.8 16.8 %copy.22 = f32[8,16,4096]{0,1,2:T(8,128)} copy(f32[8,16,4096]{2,1,0:T(8,128)S(1)} %fusion.11) | data formatting | bytes 4194304
  477.6 23.7 %reshape.56 = f32[4096,128]{1,0:T(8,128)} reshape(f32[4096,16,8]{2,1,0:T(8,128)} %bitcast.25) | data formatting | bytes 4194304
  501.7 124.2 %psum.29 = f32[8,16]{1,0:T(8,128)S(1)} all-reduce(f32[8,16]{1,0:T(8,128)S(1)} %fusion.9), channel_id=1, replica_groups=mesh['mp'=64,'head'=4] {'mp'}, use_global_device_ids=true, to_apply=%region_6.7 | all-reduce | flops 128 | bytes 1024 | tf_op jit(solution)/shard_map/psum | solution.py:44
  626.0 14.1 %reduce-scatter.4.cloned.1.call-done = f32[64,128]{1,0:T(8,128)} async-done(((f32[4096,128]{1,0:T(8,128)}), f32[64,128]{1,0:T(8,128)}) %reduce-scatter.4.cloned.1.call-update) | async-done | bytes 32784
  640.1 1.0 reshape.57
  641.6 246.1 %psum.30 = bf16[8,16,64]{2,0,1:T(8,128)(2,1)S(1)} all-reduce(f32[8,16,64]{2,0,1:T(8,128)S(1)} %convolution_bitcast_fusion), channel_id=1, replica_groups=mesh['mp'=64,'head'=4] {'mp'}, use_global_device_ids=true, to_apply=%region_7.8 | all-reduce | flops 8192 | bytes 49152 | tf_op jit(solution)/shard_map/psum | solution.py:56
  888.0 10.5 %psum.31 = f32[8,64]{1,0:T(8,128)S(1)} all-reduce(f32[8,64]{1,0:T(8,128)S(1)} %fusion.25), channel_id=1, replica_groups=mesh['mp'=64,'head'=4] {'head'}, use_global_device_ids=true, to_apply=%region_8.9 | all-reduce | flops 512 | bytes 4096 | tf_op jit(solution)/shard_map/psum | solution.py:57
  898.5 0.7 add_convert_fusion
  (27 shorter events, 1.6 us)
Async XLA Ops:
  6.5 2.7 copy-start
  271.6 17.2 %copy-start.5 = (s32[8]{0:T(128)S(1)}, s32[8]{0:T(128)}, u32[]{:S(2)}) copy-start(s32[8]{0:T(128)} %param.19) | copy-start | bytes 100
  284.0 33.5 %all-to-all-start = ((bf16[64,2,4096]{2,1,0:T(2,128)(2,1)}), bf16[64,2,4096]{2,1,0:T(2,128)(2,1)S(1)}, u32[]{:S(2)}, u32[]{:S(2)}) async-start(bf16[64,2,4096]{2,1,0:T(2,128)(2,1)} %reshape.58), calls=%async_computation | async-start | bytes 2097152 | tf_op jit(solution)/shard_map/all_to_all | solution.py:32
  288.7 351.4 %reduce-scatter.4.cloned.1.call-start = ((), (), s32[]{:S(2)}) async-start(), calls=%async_computation.2 | async-start | bytes 2129920
  325.1 7.3 copy-start.3
  325.1 7.3 copy-start.4
  477.6 23.7 %copy-start.1 = (bf16[64,1024]{1,0:T(8,128)(2,1)S(1)}, bf16[64,1024]{1,0:T(8,128)(2,1)}, u32[]{:S(2)}) copy-start(bf16[64,1024]{1,0:T(8,128)(2,1)} %param.15) | copy-start | bytes 393220
  501.3 386.6 %copy-start.2 = (bf16[1024,64]{0,1:T(8,128)(2,1)S(1)}, bf16[1024,64]{0,1:T(8,128)(2,1)}, u32[]{:S(2)}) copy-start(bf16[1024,64]{0,1:T(8,128)(2,1)} %param.16) | copy-start | bytes 393220
Sparse Core Ops, SparseCore 0:
  501.5 138.5 reduce-scatter.3

commit v2 on v0

--- a/solution.py
+++ b/solution.py
@@ -5,6 +5,10 @@
 
 EPSILON = 1e-06
 NEGATIVE = -1e30
+
+
+def register_classes_on(own_rows):
+    return jnp.sum(lax.all_gather(own_rows, axis_name="mp"), axis=0)
 
 
 def shards(
@@ -52,7 +56,7 @@
         w_value.reshape(rows, heads, head_size),
         preferred_element_type=jnp.float32,
     )
-    context = lax.psum(context, "mp").astype(jnp.bfloat16).reshape(batch, inner)
+    context = register_classes_on(context).astype(jnp.bfloat16).reshape(batch, inner)
     out = lax.psum(jnp.dot(context, w_out, preferred_element_type=jnp.float32), "head")
     cols = w_out.shape[1]
     residual = lax.dynamic_slice_in_dim(widened, me * cols, cols, 1)

time: 924 us -> 757 us (0.82)
  blocking collectives: 759 us -> 513 us
  waiting for transfers between devices: 90.8 us -> 166 us
    psum x1 -> x0, blocking collectives: 246 us -> none  [shards(): context = lax.psum(context, 'mp').astype(jnp.bfloat16).reshape(batch, inner)]
    all_gather x0 -> x1, waiting for transfers between devices: none -> 74.8 us  [register_classes_on(): return jnp.sum(lax.all_gather(own_rows, axis_name='mp'), axis=0)]
  transfers between devices with their start and end apart: 2 -> 3, of which waited for: 2 -> 3; matrix products, arithmetic and copies ran while one was open for 0% -> 0% of each run, Pallas kernels for 0% -> 0%
where the time goes in v2:
time: 757 us; the launch traced here: 754 us
  blocking collectives  513 us (68%)
  waiting for transfers between devices  166 us (22%)
  local copies, waits for them, and re-layouts  45 us (6%)
  between operations  13.2 us (2%)
  matrix products  12 us (2%)
    psum x1, blocking collectives, shards(): lax.psum(query, 'mp').astype(jnp.bfloat16).reshape(batch, heads, head_size)  252 us
    pmax x1, blocking collectives, shards(): top = lax.pmax(jnp.max(scores, axis=-1), 'mp')  126 us
    psum x1, blocking collectives, shards(): total = lax.psum(jnp.sum(weights, axis=-1), 'mp')  124 us
    all_gather x1, waiting for transfers between devices, shards(): probe = lax.all_gather(probe, 'mp', axis=2, tiled=True)  77.1 us
    all_gather x1, waiting for transfers between devices, register_classes_on(): return jnp.sum(lax.all_gather(own_rows, axis_name='mp'), axis=0)  74.8 us
    unnamed x14, local copies, waits for them, and re-layouts  41.8 us
  transfers between devices with their start and end apart: 3, of which 3 were waited for; matrix products, arithmetic and copies ran while one was open for 0% of the time, Pallas kernels for 0%

profile of v2, /device:TPU:0, one launch (start us, length us, event | category | flops | bytes accessed | tf_op | source)
XLA Modules:
  0.0 754.3 jit_solution(3215103407128692392)
XLA Ops:
  6.5 0.9 convert_element_type.32
  7.4 1.0 multiply_reduce_fusion
  8.4 0.8 dynamic-slice
  9.4 251.9 %psum.21 = bf16[8,1024]{1,0:T(8,128)(2,1)S(1)} all-reduce(f32[8,1024]{1,0:T(8,128)S(1)} %fusion.19), channel_id=1, replica_groups=mesh['mp'=64,'head'=4] {'mp'}, use_global_device_ids=true, to_apply=%region_1.0 | all-reduce | flops 8192 | bytes 49152 | tf_op jit(solution)/shard_map/psum | solution.py:27
  261.4 1.1 reshape.52
  262.5 0.3 fusion.5
  262.7 0.8 copy.17
  263.6 0.7 broadcast_compare_fusion
  264.4 77.1 %all-gather.4.cloned.1.call-done = bf16[8,16,4096]{1,0,2:T(8,128)(2,1)} async-done(((bf16[8,16,64]{1,0,2:T(8,128)(2,1)}), bf16[8,16,4096]{1,0,2:T(8,128)(2,1)}) %all-gather.4.cloned.1.call-update) | async-done | bytes 1048592 | tf_op jit(solution)/shard_map/all_gather | solution.py:35
  341.5 7.3 fusion
  348.8 0.3 fusion.24
  349.1 126.0 %pmax.7 = f32[8,16]{1,0:T(8,128)S(1)} all-reduce(f32[8,16]{1,0:T(8,128)S(1)} %get-tuple-element.5), channel_id=1, replica_groups=mesh['mp'=64,'head'=4] {'mp'}, use_global_device_ids=true, to_apply=%region_3.4 | all-reduce | flops 128 | bytes 1024 | tf_op jit(solution)/shard_map/pmax | solution.py:45
  475.1 2.9 fusion.11
  478.0 16.8 %copy.23 = f32[8,16,4096]{0,1,2:T(8,128)} copy(f32[8,16,4096]{2,1,0:T(8,128)S(1)} %fusion.11) | data formatting | bytes 4194304
  494.8 23.7 %reshape.56 = f32[4096,128]{1,0:T(8,128)} reshape(f32[4096,16,8]{2,1,0:T(8,128)} %bitcast.25) | data formatting | bytes 4194304
  519.0 124.3 %psum.22 = f32[8,16]{1,0:T(8,128)S(1)} all-reduce(f32[8,16]{1,0:T(8,128)S(1)} %fusion.9), channel_id=1, replica_groups=mesh['mp'=64,'head'=4] {'mp'}, use_global_device_ids=true, to_apply=%region_6.7 | all-reduce | flops 128 | bytes 1024 | tf_op jit(solution)/shard_map/psum | solution.py:47
  643.4 13.6 %reduce-scatter.4.cloned.1.call-done = f32[64,128]{1,0:T(8,128)} async-done(((f32[4096,128]{1,0:T(8,128)}), f32[64,128]{1,0:T(8,128)}) %reduce-scatter.4.cloned.1.call-update) | async-done | bytes 32784
  657.0 1.0 reshape.57
  658.0 0.3 copy.24
  658.3 0.9 convolution_bitcast_fusion
  659.2 74.8 %all-gather.6.cloned.1.call-done = f32[512,16,64]{2,0,1:T(8,128)} async-done(((f32[8,16,64]{2,0,1:T(8,128)}), f32[512,16,64]{2,0,1:T(8,128)}) %all-gather.6.cloned.1.call-update) | async-done | bytes 2097168 | tf_op jit(solution)/shard_map/all_gather | solution.py:11
  734.0 2.5 bitcast_reduce_fusion
  736.7 10.5 %psum.23 = f32[8,64]{1,0:T(8,128)S(1)} all-reduce(f32[8,64]{1,0:T(8,128)S(1)} %fusion.25), channel_id=1, replica_groups=mesh['mp'=64,'head'=4] {'head'}, use_global_device_ids=true, to_apply=%region_8.9 | all-reduce | flops 512 | bytes 4096 | tf_op jit(solution)/shard_map/psum | solution.py:60
  747.2 0.7 add_convert_fusion
  (26 shorter events, 1.1 us)
Async XLA Ops:
  6.5 2.7 copy-start
  6.5 334.9 %all-gather.4.cloned.1.call-start = ((), (), s32[]{:S(2)}) async-start(), calls=%async_computation.1 | async-start | bytes 8519680 | tf_op jit(solution)/shard_map/all_gather | solution.py:35
  263.6 393.4 %reduce-scatter.4.cloned.1.call-start = ((), (), s32[]{:S(2)}) async-start(), calls=%async_computation.3 | async-start | bytes 2129920
  264.4 84.4 %copy-start.3 = (f32[32,16]{0,1:T(8,128)S(1)}, f32[32,16]{0,1:T(8,128)}, u32[]{:S(2)}) copy-start(f32[32,16]{0,1:T(8,128)} %param.17) | copy-start | bytes 6148
  264.4 84.4 %copy-start.4 = (s32[8,64]{1,0:T(8,128)S(1)}, s32[8,64]{1,0:T(8,128)}, u32[]{:S(2)}) copy-start(s32[8,64]{1,0:T(8,128)} %param.18) | copy-start | bytes 6148
  494.8 23.8 %copy-start.1 = (bf16[64,1024]{1,0:T(8,128)(2,1)S(1)}, bf16[64,1024]{1,0:T(8,128)(2,1)}, u32[]{:S(2)}) copy-start(bf16[64,1024]{1,0:T(8,128)(2,1)} %param.15) | copy-start | bytes 393220
  518.5 218.0 %copy-start.2 = (bf16[1024,64]{0,1:T(8,128)(2,1)S(1)}, bf16[1024,64]{0,1:T(8,128)(2,1)}, u32[]{:S(2)}) copy-start(bf16[1024,64]{0,1:T(8,128)(2,1)} %param.16) | copy-start | bytes 393220
  518.5 215.4 %all-gather.6.cloned.1.call-start = ((), (), s32[]{:S(2)}) async-start(), calls=%async_computation.2 | async-start | bytes 4259840 | tf_op jit(solution)/shard_map/all_gather | solution.py:11
Sparse Core Ops, SparseCore 0:
  263.7 77.7 all-gather.3
  518.7 138.2 reduce-scatter.3
  659.6 74.3 all-gather.5
